TPU v7x, 512 devices: a 8x2x16 block of a 8x8x16 slice. The times are simulated.
512 devices in a mesh: groups: 2 (over y), expert: 16 (over z), split: 8 (over x), pair: 2 (over core).
Axes of the slice: x: 8, y: 2, z: 16, core: 2. Of those that a mesh axis runs over, the one named last changes fastest.
The devices are a block of a 8x8x16 slice.
Arguments:
- tokens: bfloat16 [256, 3584], P(('groups', 'expert'), ('split', 'pair')), parts along dimension 0, may hold values from -6 to 6
- routes: int32 [256, 8], P(('groups', 'expert')), parts along dimension 0, may hold values from 0 to 15, all different within a row; in each aligned block of 8 rows (0 to 7, 8 to 15, ...) at most 8 rows name the same one
- combine: float32 [256, 8], P(('groups', 'expert')), parts along dimension 0, may hold values from 0.05 to 1
- home: int32 [16], replicated, may hold values from 0 to 15, each once
- gate_up: bfloat16 [16, 3584, 2, 2560], P('expert', 'pair', None, 'split'), may hold values from -0.09375 to 0.09375
- down: bfloat16 [16, 2560, 3584], P('expert', ('split', 'pair')), may hold values from -0.15625 to 0.15625
Outputs:
- mixed: bfloat16 [256, 3584], P(('groups', 'expert'), ('split', 'pair')), parts along dimension 0
There are 2 independent parts, one for each index of `groups`. A program takes and returns all parts, laid end to end along the dimension named above; an argument that names none is the same for every part. Nothing has to cross between parts.
Inputs may be any that keep to these rules, and one draw needn't show every extreme that they name: `routes`: each row names 8 different experts. In the rows of one device no expert is named more than 8 times, and some expert reaches 8 in every draw. A permutation: expert e is held in storage slot home[e].
All inputs are finite; a program needn't handle non-finite values.
Results may differ from a plain program's by a relative error of at most 0.025.
Values may be sent and summed in bfloat16 or wider, within the bound.
No kernel may reach another device: no remote copies, remote signals or barrier semaphores. Data moves between devices by JAX's collectives and lax.ppermute only.
A program may use at most 64 MiB of HBM per device.

v0:
```python
import jax
import jax.numpy as jnp
from jax import lax
from jax.sharding import PartitionSpec as P


def in_blocks(shard, dim, length):
    before, after = (shard.shape[:dim], shard.shape[dim + 1 :])
    return jnp.moveaxis(shard.reshape(*before, length, -1, *after), dim, 0)


def summed_on_arrival(shard, axis, dim):
    pieces = in_blocks(shard, dim, lax.axis_size(axis))
    arrived = lax.all_to_all(pieces, axis, split_axis=0, concat_axis=0, tiled=True)
    return arrived.astype(jnp.float32).sum(axis=0)


def shards(tokens, routes, combine, home, gate_up, down):
    n_expert = lax.axis_size("expert")
    local_tokens = tokens.shape[0]
    chosen_count = routes.shape[1]
    experts_all = home.shape[0]
    experts_here = gate_up.shape[0]
    total_rows = experts_all * local_tokens
    width = gate_up.shape[1] * 2
    table_ids = jnp.arange(experts_all, dtype=jnp.int32)
    slot = jnp.sum(
        jnp.where(routes[:, :, None] == table_ids[None, None, :], home[None, None, :], 0), axis=-1
    )
    flat_slot = slot.reshape(-1)
    entries = flat_slot.shape[0]
    order_ids = jnp.arange(entries, dtype=jnp.int32)
    earlier = (flat_slot[:, None] == flat_slot[None, :]) & (order_ids[None, :] < order_ids[:, None])
    position = jnp.sum(earlier.astype(jnp.int32), axis=1)
    target = (flat_slot * local_tokens + position).reshape(local_tokens, chosen_count)
    row_ids = jnp.arange(total_rows, dtype=jnp.int32)
    hits = target[None, :, :] == row_ids[:, None, None]
    placing = jnp.sum(hits.astype(jnp.int32), axis=-1).astype(jnp.bfloat16)
    mixing = jnp.sum(jnp.where(hits, combine[None, :, :], jnp.float32(0.0)), axis=-1).T
    outgoing = jnp.dot(placing, tokens, preferred_element_type=jnp.float32).astype(jnp.bfloat16)
    arrived = lax.all_to_all(outgoing, "expert", split_axis=0, concat_axis=0, tiled=True)
    gathered = lax.all_gather(arrived, ("split", "pair"), axis=1, tiled=True)
    rows_each = n_expert * local_tokens
    inputs = gathered.reshape(n_expert, experts_here, local_tokens, width)
    inputs = jnp.swapaxes(inputs, 0, 1).reshape(experts_here, rows_each, width)
    pair_index = lax.axis_index("pair")
    half_width = gate_up.shape[1]
    own_half = lax.dynamic_slice_in_dim(inputs, pair_index * half_width, half_width, 2)
    before = jnp.einsum("erd,edgf->ergf", own_half, gate_up, preferred_element_type=jnp.float32)
    before = summed_on_arrival(before.astype(jnp.bfloat16), "pair", 3)
    hidden = (jax.nn.silu(before[:, :, 0, :]) * before[:, :, 1, :]).astype(jnp.bfloat16)
    partial_value = jnp.einsum(
        "erf,efd->erd", hidden, down, preferred_element_type=jnp.float32
    ).astype(jnp.bfloat16)
    summed = summed_on_arrival(partial_value, ("split", "pair"), 2).astype(jnp.bfloat16)
    narrow = summed.shape[2]
    returning = jnp.swapaxes(summed.reshape(experts_here, n_expert, local_tokens, narrow), 0, 1)
    returning = returning.reshape(total_rows, narrow)
    results = lax.all_to_all(returning, "expert", split_axis=0, concat_axis=0, tiled=True)
    mixed = jnp.dot(mixing, results.astype(jnp.float32), precision=lax.Precision.HIGHEST)
    return mixed.astype(jnp.bfloat16)


def solution(mesh):
    placed = (
        P(("groups", "expert"), ("split", "pair")),
        P(("groups", "expert"), None),
        P(("groups", "expert"), None),
        P(),
        P("expert", "pair", None, "split"),
        P("expert", ("split", "pair"), None),
    )
    return jax.shard_map(
        shards,
        mesh=mesh,
        in_specs=placed,
        out_specs=P(("groups", "expert"), ("split", "pair")),
        check_vma=False,
    )
```

profile of v0, /device:TPU:65, one launch (start us, length us, event | category | flops | bytes accessed | tf_op | source)
XLA Modules:
  0.0 136.0 jit_solution(16381093702954232302)
XLA Ops:
  0.0 0.0 copy-start
  0.0 1.1 select_reduce_fusion.1
  1.1 0.1 eq.44
  1.2 0.2 convert_reduce_fusion.2
  1.4 0.1 reduce_sum.63
  1.5 0.1 convert_reduce_fusion.1
  1.6 0.9 convolution_convert_fusion.1
  2.5 0.7 copy.25
  3.3 44.2 %all-to-all-start = ((bf16[16,8,224]{2,1,0:T(8,128)(2,1)}), bf16[16,8,224]{2,1,0:T(8,128)(2,1)S(1)}, u32[]{:S(2)}, u32[]{:S(2)}) async-start(bf16[16,8,224]{2,1,0:T(8,128)(2,1)} %bitcast), calls=%async_computation | async-start | bytes 131072 | tf_op jit(solution)/shard_map/all_to_all | solution.py:41
  47.5 11.4 %all-to-all-done = bf16[16,8,224]{2,1,0:T(8,128)(2,1)S(1)} async-done(((bf16[16,8,224]{2,1,0:T(8,128)(2,1)}), bf16[16,8,224]{2,1,0:T(8,128)(2,1)S(1)}, u32[]{:S(2)}, u32[]{:S(2)}) %all-to-all-start) | async-done | bytes 57376 | tf_op jit(solution)/shard_map/all_to_all | solution.py:41
  58.9 0.1 copy.26
  59.0 22.6 %all_gather.3 = bf16[128,3584]{0,1:T(8,128)(2,1)S(1)} all-gather(bf16[128,224]{0,1:T(8,128)(2,1)S(1)} %copy.26), channel_id=1, replica_groups=mesh['groups'=2,'expert'=16,'split'=8,'pair'=2] {'split','pair'}, dimensions={1}, use_global_device_ids=true | all-gather | bytes 974848 | tf_op jit(solution)/shard_map/all_gather | solution.py:42
  81.5 0.0 copy-done
  81.5 0.0 copy-start.1
  81.5 0.8 fusion.2
  82.3 3.7 %all_to_all.34 = bf16[2,1,128,2,160]{2,4,3,1,0:T(8,128)(2,1)S(1)} all-to-all(bf16[2,1,128,2,160]{2,4,3,1,0:T(8,128)(2,1)S(1)} %bitcast.37), channel_id=1, replica_groups=mesh['groups'=2,'expert'=16,'split'=8,'pair'=2] {'pair'}, dimensions={0} | all-to-all | bytes 327680 | tf_op jit(solution)/shard_map/all_to_all | solution.py:14
  86.0 0.0 copy-done.1
  86.0 1.4 %convolution_convert_fusion = bf16[128,3584]{1,0:T(8,128)(2,1)} fusion(bf16[1,160,3584]{2,1,0:T(8,128)(2,1)S(1)} %copy-done.1, f32[1,128,2,160]{1,3,2,0:T(8,128)S(1)} %bitcast.38), kind=kOutput, calls=%fused_computation | convolution fusion | flops 147382272 | bytes 2228224 | tf_op jit(solution)/shard_map/erf,efd->erd/dot_general | solution.py:52
  87.4 1.5 %copy.29 = bf16[128,3584]{0,1:T(8,128)(2,1)S(1)} copy(bf16[128,3584]{1,0:T(8,128)(2,1)} %convolution_convert_fusion) | data formatting | bytes 1835008 | tf_op jit(solution)/shard_map/convert_element_type | solution.py:54
  88.9 0.0 copy-start.2
  89.0 30.0 %all_to_all.35 = bf16[16,1,128,224]{2,3,1,0:T(8,128)(2,1)S(1)} all-to-all(bf16[16,1,128,224]{2,3,1,0:T(8,128)(2,1)S(1)} %bitcast.35), channel_id=1, replica_groups=mesh['groups'=2,'expert'=16,'split'=8,'pair'=2] {'split','pair'}, dimensions={0} | all-to-all | bytes 1835008 | tf_op jit(solution)/shard_map/all_to_all | solution.py:14
  119.0 0.1 bitcast_reduce_fusion
  119.1 0.7 copy.32
  119.9 3.9 %all-to-all-start.3 = ((bf16[16,8,224]{2,1,0:T(8,128)(2,1)}), bf16[16,8,224]{2,1,0:T(8,128)(2,1)S(1)}, u32[]{:S(2)}, u32[]{:S(2)}) async-start(bf16[16,8,224]{2,1,0:T(8,128)(2,1)} %bitcast.13), calls=%async_computation.3 | async-start | bytes 131072 | tf_op jit(solution)/shard_map/all_to_all | solution.py:59
  123.8 0.0 copy-done.2
  123.8 0.1 select_reduce_fusion
  123.9 11.4 %all-to-all-done.3 = bf16[16,8,224]{2,1,0:T(8,128)(2,1)S(1)} async-done(((bf16[16,8,224]{2,1,0:T(8,128)(2,1)}), bf16[16,8,224]{2,1,0:T(8,128)(2,1)S(1)}, u32[]{:S(2)}, u32[]{:S(2)}) %all-to-all-start.3) | async-done | bytes 57376 | tf_op jit(solution)/shard_map/all_to_all | solution.py:59
  135.3 0.7 convolution_convert_fusion.2
  (3 shorter events, 0.0 us)
Async XLA Ops:
  0.0 81.5 %copy-start = (bf16[1,1792,2,320]{1,3,2,0:T(8,128)(2,1)S(1)}, bf16[1,1792,2,320]{1,3,2,0:T(8,128)(2,1)}, u32[]{:S(2)}) copy-start(bf16[1,1792,2,320]{1,3,2,0:T(8,128)(2,1)} %param.10) | copy-start | bytes 6881284
  3.3 55.6 %all-to-all-start = ((bf16[16,8,224]{2,1,0:T(8,128)(2,1)}), bf16[16,8,224]{2,1,0:T(8,128)(2,1)S(1)}, u32[]{:S(2)}, u32[]{:S(2)}) async-start(bf16[16,8,224]{2,1,0:T(8,128)(2,1)} %bitcast), calls=%async_computation | async-start | bytes 131072 | tf_op jit(solution)/shard_map/all_to_all | solution.py:41
  81.5 4.5 %copy-start.1 = (bf16[1,160,3584]{2,1,0:T(8,128)(2,1)S(1)}, bf16[1,160,3584]{2,1,0:T(8,128)(2,1)}, u32[]{:S(2)}) copy-start(bf16[1,160,3584]{2,1,0:T(8,128)(2,1)} %param.11) | copy-start | bytes 3440644
  88.9 34.9 %copy-start.2 = (f32[8,8]{1,0:T(8,128)S(1)}, f32[8,8]{1,0:T(8,128)}, u32[]{:S(2)}) copy-start(f32[8,8]{1,0:T(8,128)} %param.8) | copy-start | bytes 772
  119.9 15.4 %all-to-all-start.3 = ((bf16[16,8,224]{2,1,0:T(8,128)(2,1)}), bf16[16,8,224]{2,1,0:T(8,128)(2,1)S(1)}, u32[]{:S(2)}, u32[]{:S(2)}) async-start(bf16[16,8,224]{2,1,0:T(8,128)(2,1)} %bitcast.13), calls=%async_computation.3 | async-start | bytes 131072 | tf_op jit(solution)/shard_map/all_to_all | solution.py:59
where the time goes:
time: 136 us
  blocking collectives  56.3 us (41%)
  starting transfers between devices  48.2 us (35%)
  waiting for transfers between devices  22.8 us (17%)
  matrix products  3.8 us (3%)
  local copies, waits for them, and re-layouts  3.3 us (2%)
  other arithmetic  1.66 us (1%)
    all_to_all x1, starting transfers between devices, shards(): lax.all_to_all(outgoing, 'expert', split_axis=0, concat_axis=0, tiled=True)  44.2 us
    all_to_all x2, blocking collectives, summed_on_arrival(): lax.all_to_all(pieces, axis, split_axis=0, concat_axis=0, tiled=True)  33.7 us
    all_gather x1, blocking collectives, shards(): gathered = lax.all_gather(arrived, ('split', 'pair'), axis=1, tiled=True)  22.6 us
    all_to_all x1, waiting for transfers between devices, shards(): lax.all_to_all(returning, 'expert', split_axis=0, concat_axis=0, tiled=True)  11.4 us
    all_to_all x1, waiting for transfers between devices, shards(): lax.all_to_all(outgoing, 'expert', split_axis=0, concat_axis=0, tiled=True)  11.4 us
    all_to_all x1, starting transfers between devices, shards(): lax.all_to_all(returning, 'expert', split_axis=0, concat_axis=0, tiled=True)  3.94 us
  transfers between devices with their start and end apart: 2, of which 2 were waited for; matrix products, arithmetic and copies ran while one was open for 0% of the time, Pallas kernels for 0%

commit v1 on v0

v1 whole, which is shorter than its diff:
```python
import jax
import jax.numpy as jnp
from jax import lax
from jax.experimental import pallas as pl
from jax.experimental.pallas import tpu as pltpu
from jax.sharding import PartitionSpec as P

VMEM = pl.BlockSpec(memory_space=pltpu.VMEM)
SMEM = pl.BlockSpec(memory_space=pltpu.SMEM)
LANES = 128


def padded(value, lanes):
    rows, width = value.shape
    if width == lanes:
        return value
    return jnp.concatenate([value, jnp.zeros((rows, lanes - width), value.dtype)], axis=1)


def dispatch_kernel(home_ref, tokens_ref, routes_ref, combine_ref, out_ref):
    slots, rows, lanes = out_ref.shape
    width = tokens_ref.shape[1]
    routes = routes_ref[...]
    combine = combine_ref[...]
    slot = jnp.zeros_like(routes)
    for expert in range(slots):
        slot = jnp.where(routes == expert, home_ref[expert], slot)
    tokens = padded(tokens_ref[...].astype(jnp.float32), lanes)
    lane = lax.broadcasted_iota(jnp.int32, (rows, lanes), 1)
    for s in range(slots):
        weight = jnp.sum(jnp.where(slot == s, combine, 0.0), axis=1, keepdims=True)
        high = weight.astype(jnp.bfloat16).astype(jnp.float32)
        value = jnp.where(lane == width, high, jnp.where(lane == width + 1, weight - high, tokens))
        out_ref[s] = value.astype(jnp.bfloat16)


def arrange_kernel(pair_ref, up_ref, down_ref, up_keep, up_send, down_keep, down_send, *, width):
    even = pair_ref[0] == 0
    lanes = up_keep.shape[2]
    for ref, keep, send in ((up_ref, up_keep, up_send), (down_ref, down_keep, down_send)):
        for i in range(keep.shape[0]):
            first = padded(ref[:, 2 * i * width : (2 * i + 1) * width], lanes)
            second = padded(ref[:, (2 * i + 1) * width : (2 * i + 2) * width], lanes)
            keep[i] = jnp.where(even, first, second)
            send[i] = jnp.where(even, second, first)


def before_kernel(pair_ref, x_ref, keep_ref, recv_ref, out_ref):
    pair = pair_ref[0]
    blocks = keep_ref.shape[0]
    total = None
    for i in range(blocks):
        for ref, half in ((keep_ref, pair), (recv_ref, 1 - pair)):
            part = lax.dot_general(
                x_ref[half * blocks + i], ref[i], (((1,), (1,)), ((), ())), preferred_element_type=jnp.float32
            )
            total = part if total is None else total + part
    out_ref[...] = total.astype(out_ref.dtype)


def after_kernel(pair_ref, own_ref, other_ref, payload_ref, keep_ref, recv_ref, out_ref, *, width):
    even = pair_ref[0] == 0
    before = own_ref[...].astype(jnp.float32) + other_ref[...].astype(jnp.float32)
    units = before.shape[1] // 2
    gate, up = before[:, :units], before[:, units:]
    weight = payload_ref[:, width : width + 2].astype(jnp.float32)
    weight = weight[:, 0:1] + weight[:, 1:2]
    hidden = (gate / (1.0 + jnp.exp(-gate)) * up * weight).astype(jnp.bfloat16)
    low, high = hidden[:, : units // 2], hidden[:, units // 2 :]
    own = jnp.where(even, low, high)
    other = jnp.where(even, high, low)
    for i in range(out_ref.shape[0]):
        part = jnp.dot(own, keep_ref[i], preferred_element_type=jnp.float32)
        part = part + jnp.dot(other, recv_ref[i], preferred_element_type=jnp.float32)
        out_ref[i] = part.astype(out_ref.dtype)


def call(kernel, outs, specs, *operands):
    shapes = [jax.ShapeDtypeStruct(shape, jnp.bfloat16) for shape in outs]
    single = len(shapes) == 1
    return pl.pallas_call(
        kernel,
        out_shape=shapes[0] if single else shapes,
        in_specs=specs,
        out_specs=VMEM if single else [VMEM] * len(shapes),
    )(*operands)


def experts(tokens, routes, combine, home, gate_up, down):
    n_expert, n_split, n_pair = (lax.axis_size(name) for name in ("expert", "split", "pair"))
    rows, width = tokens.shape
    lanes = -(-(width + 2) // LANES) * LANES
    features = gate_up.shape[1]
    units = gate_up.shape[3]
    total_rows = n_expert * rows
    pair = lax.axis_index("pair").astype(jnp.int32).reshape(1)
    swap = [(0, 1), (1, 0)]

    payload = call(
        dispatch_kernel, [(n_expert, rows, lanes)], [SMEM, VMEM, VMEM, VMEM], home, tokens, routes, combine
    )
    arrived = lax.all_to_all(payload, "expert", split_axis=0, concat_axis=0, tiled=True)

    up_rows = jnp.transpose(gate_up[0], (1, 2, 0)).reshape(2 * units, features)
    down_rows = down[0]
    half_blocks = n_split // n_pair
    up_keep, up_send, down_keep, down_send = call(
        lambda *refs: arrange_kernel(*refs, width=width),
        [(half_blocks, 2 * units, lanes)] * 2 + [(n_split, down_rows.shape[0], lanes)] * 2,
        [SMEM, VMEM, VMEM],
        pair,
        up_rows,
        down_rows,
    )
    up_recv = lax.ppermute(up_send, "pair", swap)
    down_recv = lax.ppermute(down_send, "pair", swap)

    arrived = arrived.reshape(total_rows, lanes)
    spread = jnp.broadcast_to(arrived[None], (n_split, total_rows, lanes))
    gathered = lax.all_to_all(spread, "split", split_axis=0, concat_axis=0, tiled=True)
    own = call(
        before_kernel, [(total_rows, 2 * units)], [SMEM, VMEM, VMEM, VMEM], pair, gathered, up_keep, up_recv
    )
    other = lax.ppermute(own, "pair", swap)
    partial = call(
        lambda *refs: after_kernel(*refs, width=width),
        [(n_split, total_rows, lanes)],
        [SMEM] + [VMEM] * 5,
        pair,
        own,
        other,
        arrived,
        down_keep,
        down_recv,
    )
    parts = lax.all_to_all(partial, "split", split_axis=0, concat_axis=0, tiled=True)
    summed = parts.astype(jnp.float32).sum(axis=0).astype(jnp.bfloat16)
    returning = summed.reshape(n_expert, rows, lanes)
    results = lax.all_to_all(returning, "expert", split_axis=0, concat_axis=0, tiled=True)
    mixed = results.astype(jnp.float32).sum(axis=0)
    return mixed[:, :width].astype(jnp.bfloat16)


def solution(mesh):
    placed = (
        P(("groups", "expert"), ("split", "pair")),
        P(("groups", "expert"), None),
        P(("groups", "expert"), None),
        P(),
        P("expert", "pair", None, "split"),
        P("expert", ("split", "pair"), None),
    )
    return jax.shard_map(
        experts,
        mesh=mesh,
        in_specs=placed,
        out_specs=P(("groups", "expert"), ("split", "pair")),
        check_vma=False,
    )
```

time: 136 us -> 141 us (1.037); the launches traced: 136 us -> 140 us
  Pallas kernels: 0 us -> 12.5 us
  starting transfers between devices: 48.2 us -> 59.6 us
  waiting for transfers between devices: 22.8 us -> 12.2 us
  blocking collectives: 56.3 us -> 51.9 us
  matrix products: 3.8 us -> 0 us
    ppermute x0 -> x3, starting transfers between devices: none -> 52.9 us  [the longest x1 43.5 us: experts(): up_recv = lax.ppermute(up_send, 'pair', swap)]
    all_to_all x2 -> x1, starting transfers between devices: 48.2 us -> 6.71 us  [experts(): lax.all_to_all(spread, 'split', split_axis=0, concat_axis=0, tiled=True)]
    all_gather x1 -> x0, blocking collectives: 22.6 us -> none  [shards(): gathered = lax.all_gather(arrived, ('split', 'pair'), axis=1, tiled=True)]
    all_to_all x2 -> x3, blocking collectives: 33.7 us -> 51.9 us  [the longest x1 21.4 us: experts(): lax.all_to_all(partial, 'split', split_axis=0, concat_axis=0, tiled=True)]
    pallas_call x0 -> x4, Pallas kernels: none -> 12.5 us  [call(): pl.pallas_call(kernel, out_shape=shapes[0] if single else shapes, in_spec...]
    all_to_all x2 -> x1, waiting for transfers between devices: 22.8 us -> 11 us  [experts(): lax.all_to_all(spread, 'split', split_axis=0, concat_axis=0, tiled=True)]
    dot_general x4 -> x0, matrix products: 3.8 us -> none  [the longest x1 1.38 us: shards(): jnp.einsum('erf,efd->erd', hidden, down, preferred_element_type=jnp.float32)]
    convert_element_type x2 -> x0, local copies, waits for them, and re-layouts: 2.29 us -> none  [the longest x1 1.55 us: shards(): partial_value = jnp.einsum('erf,efd->erd', hidden, down, preferred_elemen...]
  transfers between devices with their start and end apart: 2 -> 4, of which waited for: 2 -> 2; matrix products, arithmetic and copies ran while one was open for 0% -> 1% of each run, Pallas kernels for 0% -> 4%
where the time goes in v1:
time: 141 us; the launch traced here: 140 us
  starting transfers between devices  59.6 us (42%)
  blocking collectives  51.9 us (37%)
  Pallas kernels  12.5 us (9%)
  waiting for transfers between devices  12.2 us (9%)
  local copies, waits for them, and re-layouts  2.76 us (2%)
    ppermute x1, starting transfers between devices, experts(): up_recv = lax.ppermute(up_send, 'pair', swap)  43.5 us
    all_to_all x1, blocking collectives, experts(): lax.all_to_all(partial, 'split', split_axis=0, concat_axis=0, tiled=True)  21.4 us
    all_to_all x1, blocking collectives, experts(): lax.all_to_all(returning, 'expert', split_axis=0, concat_axis=0, tiled=True)  15.4 us
    all_to_all x1, blocking collectives, experts(): lax.all_to_all(payload, 'expert', split_axis=0, concat_axis=0, tiled=True)  15.2 us
    pallas_call x4, Pallas kernels, call(): pl.pallas_call(kernel, out_shape=shapes[0] if single else shapes, in_spec...  12.5 us
    all_to_all x1, waiting for transfers between devices, experts(): lax.all_to_all(spread, 'split', split_axis=0, concat_axis=0, tiled=True)  11 us
    all_to_all x1, starting transfers between devices, experts(): lax.all_to_all(spread, 'split', split_axis=0, concat_axis=0, tiled=True)  6.71 us
    ppermute x1, starting transfers between devices, experts(): other = lax.ppermute(own, 'pair', swap)  5.08 us
  transfers between devices with their start and end apart: 4, of which 2 were waited for; matrix products, arithmetic and copies ran while one was open for 1% of the time, Pallas kernels for 4%

profile of v1, /device:TPU:65, one launch (start us, length us, event | category | flops | bytes accessed | tf_op | source)
XLA Modules:
  0.0 139.6 jit_solution(2723624174188866086)
XLA Ops:
  0.0 4.6 %shard_map.65 = (bf16[4,640,256]{2,1,0:T(8,128)(2,1)}, bf16[4,640,256]{2,1,0:T(8,128)(2,1)}, bf16[8,160,256]{2,1,0:T(8,128)(2,1)}, bf16[8,160,256]{2,1,0:T(8,128)(2,1)}) custom-call(s32[1]{0:T(128)} %bitcast.refs_0_.pair_ref, bf16[640,1792]{1,0:T(8,128)(2,1)} %bitcast.10, bf16[160,3584]{1,0:T(8,128)(2,1)} %bitcast.11), custom_call_target="tpu_custom_call" | custom-call | tf_op jit(solution)/shard_map/pallas_call | solution.py:81
  4.6 0.0 copy-start.5
  4.6 43.5 %collective-permute-start = (bf16[4,640,256]{2,1,0:T(8,128)(2,1)}, bf16[4,640,256]{2,1,0:T(8,128)(2,1)S(1)}, u32[]{:S(2)}, u32[]{:S(2)}) collective-permute-start(bf16[4,640,256]{2,1,0:T(8,128)(2,1)} %get-tuple-element.10), channel_id=1, source_target_pairs={{0,1},{1,0},{2,3},{3,2},{4,5},{5,4},{6,7},{7,6},{8,9},{9,8},{10,11... | collective-permute-start | bytes 3932168 | tf_op jit(solution)/shard_map/ppermute | solution.py:115
  48.1 1.5 %shard_map.64 = bf16[16,8,256]{2,1,0:T(8,128)(2,1)} custom-call(s32[16]{0:T(128)} %home_ref.1, bf16[8,224]{1,0:T(8,128)(2,1)} %tokens_ref.1, s32[8,8]{1,0:T(8,128)} %routes_ref.1, f32[8,8]{1,0:T(8,128)} %combine_ref.1), custom_call_target="tpu_custom_call" | custom-call | tf_op jit(solution)/shard_map/pallas_call | solution.py:81
  49.6 15.2 %all_to_all.20 = bf16[16,8,256]{2,1,0:T(8,128)(2,1)S(1)} all-to-all(bf16[16,8,256]{2,1,0:T(8,128)(2,1)} %shard_map.64), channel_id=1, replica_groups=mesh['groups'=2,'expert'=16,'split'=8,'pair'=2] {'expert'}, dimensions={0} | all-to-all | bytes 131072 | tf_op jit(solution)/shard_map/all_to_all | solution.py:102
  64.8 0.0 copy-start.3
  64.8 0.8 broadcast_in_dim.8
  65.6 6.7 %all-to-all-start.1 = ((bf16[8,128,256]{2,1,0:T(8,128)(2,1)}), bf16[8,128,256]{2,1,0:T(8,128)(2,1)S(1)}, u32[]{:S(2)}, u32[]{:S(2)}) async-start(bf16[8,128,256]{2,1,0:T(8,128)(2,1)} %broadcast_in_dim.8), calls=%async_computation.1 | async-start | bytes 1048576 | tf_op jit(solution)/shard_map/all_to_all | solution.py:120
  72.3 0.0 copy-done.5
  72.3 4.3 %collective-permute-start.2 = (bf16[8,160,256]{2,1,0:T(8,128)(2,1)S(1)}, bf16[8,160,256]{2,1,0:T(8,128)(2,1)S(1)}, u32[]{:S(2)}, u32[]{:S(2)}) collective-permute-start(bf16[8,160,256]{2,1,0:T(8,128)(2,1)S(1)} %copy-done.5), channel_id=1, source_target_pairs={{0,1},{1,0},{2,3},{3,2},{4,5},{5,4},{6,7},{7,6},{8,9},{9,8},{10,11... | collective-permute-start | bytes 1966088 | tf_op jit(solution)/shard_map/ppermute | solution.py:116
  76.6 11.0 %all-to-all-done.1.x_ref = bf16[8,128,256]{2,1,0:T(8,128)(2,1)S(1)} async-done(((bf16[8,128,256]{2,1,0:T(8,128)(2,1)}), bf16[8,128,256]{2,1,0:T(8,128)(2,1)S(1)}, u32[]{:S(2)}, u32[]{:S(2)}) %all-to-all-start.1) | async-done | bytes 524320 | tf_op jit(solution)/shard_map/all_to_all | solution.py:120
  87.6 0.0 copy-start
  87.6 0.0 collective-permute-done.recv_ref
  87.6 0.0 copy-start.1
  87.6 0.8 copy-done
  88.4 0.4 copy-done.1
  88.9 3.4 %shard_map.66.refs_1_ = bf16[128,640]{1,0:T(8,128)(2,1)} custom-call(s32[1]{0:T(128)} %bitcast.refs_0_.pair_ref, bf16[8,128,256]{2,1,0:T(8,128)(2,1)} %copy-done, bf16[4,640,256]{2,1,0:T(8,128)(2,1)} %get-tuple-element.9.keep_ref, bf16[4,640,256]{2,1,0:T(8,128)(2,1)} %copy-done.1), custom_call_target="tpu_custom_call" | custom-call | tf_op jit(solution)/shard_map/pallas_call | solution.py:81
  92.3 0.0 copy-done.3
  92.3 5.1 %collective-permute-start.1 = (bf16[128,640]{1,0:T(8,128)(2,1)}, bf16[128,640]{1,0:T(8,128)(2,1)S(1)}, u32[]{:S(2)}, u32[]{:S(2)}) collective-permute-start(bf16[128,640]{1,0:T(8,128)(2,1)} %shard_map.66.refs_1_), channel_id=1, source_target_pairs={{0,1},{1,0},{2,3},{3,2},{4,5},{5,4},{6,7},{7,6},{8,9},{9,8},{10,11... | collective-permute-start | bytes 491528 | tf_op jit(solution)/shard_map/ppermute | solution.py:124
  97.4 0.0 collective-permute-done.2.refs_5_
  97.4 0.0 copy-start.2
  97.4 1.2 collective-permute-done.1.refs_2_
  98.6 0.0 copy-start.4
  98.6 0.0 copy-done.2
  98.6 0.7 copy-done.4
  99.2 2.9 %shard_map.67 = bf16[8,128,256]{2,1,0:T(8,128)(2,1)} custom-call(s32[1]{0:T(128)} %bitcast.refs_0_.pair_ref, bf16[128,640]{1,0:T(8,128)(2,1)} %shard_map.66.refs_1_, bf16[128,640]{1,0:T(8,128)(2,1)} %copy-done.4, bf16[128,256]{1,0:T(8,128)(2,1)} %bitcast.13, bf16[8,160,256]{2,1,0:T(8,128)(2,1)} %get-tuple-element.11.refs_4_, bf16[8,160,256]{2,1,0:T(8,128)(2,1)} %copy-done.2), custom_call_target="tpu_custom_call" | custom-call | tf_op jit(solution)/shard_map/pallas_call | solution.py:81
  102.2 21.4 %all_to_all.21 = bf16[8,128,256]{2,1,0:T(8,128)(2,1)S(1)} all-to-all(bf16[8,128,256]{2,1,0:T(8,128)(2,1)} %shard_map.67), channel_id=1, replica_groups=mesh['groups'=2,'expert'=16,'split'=8,'pair'=2] {'split'}, dimensions={0} | all-to-all | bytes 1048576 | tf_op jit(solution)/shard_map/all_to_all | solution.py:136
  123.6 0.1 reduce_sum.21
  123.6 15.4 %all_to_all.22 = bf16[16,8,256]{2,1,0:T(8,128)(2,1)S(1)} all-to-all(bf16[16,8,256]{2,1,0:T(8,128)(2,1)S(1)} %bitcast.14), channel_id=1, replica_groups=mesh['groups'=2,'expert'=16,'split'=8,'pair'=2] {'expert'}, dimensions={0} | all-to-all | bytes 131072 | tf_op jit(solution)/shard_map/all_to_all | solution.py:139
  139.0 0.6 reduce.1
Async XLA Ops:
  4.6 67.7 %copy-start.5 = (bf16[8,160,256]{2,1,0:T(8,128)(2,1)S(1)}, bf16[8,160,256]{2,1,0:T(8,128)(2,1)}, u32[]{:S(2)}) copy-start(bf16[8,160,256]{2,1,0:T(8,128)(2,1)} %get-tuple-element.12) | copy-start | bytes 1966084
  4.6 83.0 %collective-permute-start = (bf16[4,640,256]{2,1,0:T(8,128)(2,1)}, bf16[4,640,256]{2,1,0:T(8,128)(2,1)S(1)}, u32[]{:S(2)}, u32[]{:S(2)}) collective-permute-start(bf16[4,640,256]{2,1,0:T(8,128)(2,1)} %get-tuple-element.10), channel_id=1, source_target_pairs={{0,1},{1,0},{2,3},{3,2},{4,5},{5,4},{6,7},{7,6},{8,9},{9,8},{10,11... | collective-permute-start | bytes 3932168 | tf_op jit(solution)/shard_map/ppermute | solution.py:115
  64.8 27.5 %copy-start.3 = (bf16[16,8,256]{2,1,0:T(8,128)(2,1)}, bf16[16,8,256]{2,1,0:T(8,128)(2,1)S(1)}, u32[]{:S(2)}) copy-start(bf16[16,8,256]{2,1,0:T(8,128)(2,1)S(1)} %all_to_all.20) | copy-start | bytes 196612
  65.6 22.0 %all-to-all-start.1 = ((bf16[8,128,256]{2,1,0:T(8,128)(2,1)}), bf16[8,128,256]{2,1,0:T(8,128)(2,1)S(1)}, u32[]{:S(2)}, u32[]{:S(2)}) async-start(bf16[8,128,256]{2,1,0:T(8,128)(2,1)} %broadcast_in_dim.8), calls=%async_computation.1 | async-start | bytes 1048576 | tf_op jit(solution)/shard_map/all_to_all | solution.py:120
  72.3 25.0 %collective-permute-start.2 = (bf16[8,160,256]{2,1,0:T(8,128)(2,1)S(1)}, bf16[8,160,256]{2,1,0:T(8,128)(2,1)S(1)}, u32[]{:S(2)}, u32[]{:S(2)}) collective-permute-start(bf16[8,160,256]{2,1,0:T(8,128)(2,1)S(1)} %copy-done.5), channel_id=1, source_target_pairs={{0,1},{1,0},{2,3},{3,2},{4,5},{5,4},{6,7},{7,6},{8,9},{9,8},{10,11... | collective-permute-start | bytes 1966088 | tf_op jit(solution)/shard_map/ppermute | solution.py:116
  87.6 0.8 copy-start
  87.6 1.2 copy-start.1
  92.3 6.3 %collective-permute-start.1 = (bf16[128,640]{1,0:T(8,128)(2,1)}, bf16[128,640]{1,0:T(8,128)(2,1)S(1)}, u32[]{:S(2)}, u32[]{:S(2)}) collective-permute-start(bf16[128,640]{1,0:T(8,128)(2,1)} %shard_map.66.refs_1_), channel_id=1, source_target_pairs={{0,1},{1,0},{2,3},{3,2},{4,5},{5,4},{6,7},{7,6},{8,9},{9,8},{10,11... | collective-permute-start | bytes 491528 | tf_op jit(solution)/shard_map/ppermute | solution.py:124
  97.4 1.2 copy-start.2
  98.6 0.7 copy-start.4

commit v2 on v1

v2 whole, which is shorter than its diff:
```python
import jax
import jax.numpy as jnp
from jax import lax
from jax.experimental import pallas as pl
from jax.experimental.pallas import tpu as pltpu
from jax.sharding import PartitionSpec as P

VMEM = pl.BlockSpec(memory_space=pltpu.VMEM)
SMEM = pl.BlockSpec(memory_space=pltpu.SMEM)
INNER = object()
LANES = 128
GRANT = 16 << 20
BF16 = jnp.bfloat16


def padded(value, lanes):
    rows, width = value.shape
    if width == lanes:
        return value
    return jnp.concatenate([value, jnp.zeros((rows, lanes - width), value.dtype)], axis=1)


def dispatch_kernel(home_ref, tokens_ref, routes_ref, combine_ref, out_ref):
    slots, rows, lanes = out_ref.shape
    width = tokens_ref.shape[1]
    routes = routes_ref[...]
    combine = combine_ref[...]
    slot = jnp.zeros_like(routes)
    for expert in range(slots):
        slot = jnp.where(routes == expert, home_ref[expert], slot)
    tokens = padded(tokens_ref[...].astype(jnp.float32), lanes)
    lane = lax.broadcasted_iota(jnp.int32, (rows, lanes), 1)
    for s in range(slots):
        weight = jnp.sum(jnp.where(slot == s, combine, 0.0), axis=1, keepdims=True)
        high = weight.astype(jnp.bfloat16).astype(jnp.float32)
        value = jnp.where(lane == width, high, jnp.where(lane == width + 1, weight - high, tokens))
        out_ref[s] = value.astype(jnp.bfloat16)


def arrange_kernel(pair_ref, up_ref, down_ref, keep_ref, send_ref, *, width):
    even = pair_ref[0] == 0

    def cut(ref, i, turn):
        first = ref[:, 2 * i * width : (2 * i + 1) * width]
        second = ref[:, (2 * i + 1) * width : (2 * i + 2) * width]
        return (first.T, second.T) if turn else (first, second)

    row = 0
    for ref, turn in ((up_ref, False), (down_ref, True)):
        for i in range(ref.shape[1] // (2 * width)):
            first, second = cut(ref, i, turn)
            place = (pl.ds(row, first.shape[0]), pl.ds(0, first.shape[1]))
            keep_ref[place] = jnp.where(even, first, second)
            send_ref[place] = jnp.where(even, second, first)
            row += first.shape[0]


def spread_kernel(arrived_ref, x_ref, weight_ref):
    width = x_ref.shape[1]
    turned = arrived_ref[...].astype(jnp.float32).T
    tokens = turned[:width].astype(x_ref.dtype)
    for i in range(x_ref.shape[0]):
        x_ref[i] = tokens
    weight_ref[...] = turned[width : width + 1] + turned[width + 1 : width + 2]


def before_kernel(pair_ref, x_ref, keep_ref, recv_ref, out_ref):
    pair = pair_ref[0]
    blocks, width = x_ref.shape[0] // 2, x_ref.shape[1]
    rows = out_ref.shape[0]
    total = None
    for i in range(blocks):
        for ref, half in ((keep_ref, pair), (recv_ref, 1 - pair)):
            part = jnp.dot(
                ref[i * rows : (i + 1) * rows, :width],
                x_ref[half * blocks + i],
                preferred_element_type=jnp.float32,
            )
            total = part if total is None else total + part
    out_ref[...] = total.astype(out_ref.dtype)


def after_kernel(pair_ref, own_ref, other_ref, weight_ref, keep_ref, recv_ref, out_ref):
    even = pair_ref[0] == 0
    before = own_ref[...].astype(jnp.float32) + other_ref[...].astype(jnp.float32)
    units = before.shape[0] // 2
    gate, up = before[:units], before[units:]
    hidden = (gate / (1.0 + jnp.exp(-gate)) * up * weight_ref[...]).astype(jnp.bfloat16)
    depth = units // 2
    low, high = hidden[:depth], hidden[depth:]
    own = jnp.where(even, low, high)
    other = jnp.where(even, high, low)
    blocks, width, _ = out_ref.shape
    start = keep_ref.shape[0] - blocks * width
    for i in range(blocks):
        place = (pl.ds(start + i * width, width), pl.ds(0, depth))
        part = jnp.dot(keep_ref[place], own, preferred_element_type=jnp.float32)
        part = part + jnp.dot(recv_ref[place], other, preferred_element_type=jnp.float32)
        out_ref[i] = part.astype(out_ref.dtype)


def gather_kernel(parts_ref, out_ref):
    total = parts_ref[0].astype(jnp.float32)
    for i in range(1, parts_ref.shape[0]):
        total = total + parts_ref[i].astype(jnp.float32)
    out_ref[...] = total.T.astype(out_ref.dtype)


def call(kernel, outs, specs, *operands):
    outs = [pltpu.VMEM(shape, dtype) for shape, dtype in outs]
    operands = [
        pltpu.with_memory_space_constraint(operand, pltpu.VMEM) if spec is INNER else operand
        for operand, spec in zip(operands, specs)
    ]
    single = len(outs) == 1
    return pl.pallas_call(
        kernel,
        out_shape=outs[0] if single else outs,
        in_specs=[VMEM if spec is INNER else spec for spec in specs],
        out_specs=VMEM if single else [VMEM] * len(outs),
        compiler_params=pltpu.CompilerParams(vmem_limit_bytes=GRANT),
    )(*operands)


def experts(tokens, routes, combine, home, gate_up, down):
    n_expert, n_split, n_pair = (lax.axis_size(name) for name in ("expert", "split", "pair"))
    rows, width = tokens.shape
    lanes = -(-(width + 2) // LANES) * LANES
    features = gate_up.shape[1]
    units = gate_up.shape[3]
    total_rows = n_expert * rows
    pair = lax.axis_index("pair").astype(jnp.int32).reshape(1)
    swap = [(0, 1), (1, 0)]

    payload = call(
        dispatch_kernel, [((n_expert, rows, lanes), BF16)], [SMEM, VMEM, VMEM, VMEM], home, tokens, routes, combine
    )
    arrived = lax.all_to_all(payload, "expert", split_axis=0, concat_axis=0, tiled=True)

    up_rows = jnp.transpose(gate_up[0], (1, 2, 0)).reshape(2 * units, features)
    down_rows = down[0]
    arranged = (n_split // n_pair * 2 * units + n_split * width, -(-width // LANES) * LANES)
    keep, send = call(
        lambda *refs: arrange_kernel(*refs, width=width),
        [(arranged, BF16)] * 2,
        [SMEM, VMEM, VMEM],
        pair,
        up_rows,
        down_rows,
    )
    recv = lax.ppermute(send, "pair", swap)

    spread, weight = call(
        spread_kernel,
        [((n_split, width, total_rows), BF16), ((1, total_rows), jnp.float32)],
        [INNER],
        arrived.reshape(total_rows, lanes),
    )
    gathered = lax.all_to_all(spread, "split", split_axis=0, concat_axis=0, tiled=True)
    own = call(
        before_kernel,
        [((2 * units, total_rows), BF16)],
        [SMEM, INNER, INNER, INNER],
        pair,
        gathered,
        keep,
        recv,
    )
    other = lax.ppermute(own, "pair", swap)
    partial = call(
        after_kernel,
        [((n_split, width, total_rows), BF16)],
        [SMEM] + [INNER] * 5,
        pair,
        own,
        other,
        weight,
        keep,
        recv,
    )
    parts = lax.all_to_all(partial, "split", split_axis=0, concat_axis=0, tiled=True)
    returning = call(gather_kernel, [((total_rows, width), BF16)], [INNER], parts)
    results = lax.all_to_all(
        returning.reshape(n_expert, rows, width), "expert", split_axis=0, concat_axis=0, tiled=True
    )
    return results.astype(jnp.float32).sum(axis=0).astype(BF16)


def solution(mesh):
    placed = (
        P(("groups", "expert"), ("split", "pair")),
        P(("groups", "expert"), None),
        P(("groups", "expert"), None),
        P(),
        P("expert", "pair", None, "split"),
        P("expert", ("split", "pair"), None),
    )
    return jax.shard_map(
        experts,
        mesh=mesh,
        in_specs=placed,
        out_specs=P(("groups", "expert"), ("split", "pair")),
        check_vma=False,
    )
```

time: 141 us -> 130 us (0.922)
  blocking collectives: 51.9 us -> 68.7 us
  waiting for transfers between devices: 12.2 us -> 1.01 us
  starting transfers between devices: 59.6 us -> 49.4 us
  Pallas kernels: 12.5 us -> 5.66 us
    all_to_all x1 -> x2, blocking collectives: 15.4 us -> 35.1 us  [the longest x1 19.8 us: experts(): lax.all_to_all(spread, 'split', split_axis=0, concat_axis=0, tiled=True)]
    all_to_all x1 -> x0, waiting for transfers between devices: 11 us -> none  [experts(): lax.all_to_all(spread, 'split', split_axis=0, concat_axis=0, tiled=True)]
    pallas_call x4 -> x6, Pallas kernels: 12.5 us -> 5.66 us  [call(): pl.pallas_call(kernel, out_shape=outs[0] if single else outs, in_specs=[V...]
    all_to_all x1 -> x0, starting transfers between devices: 6.71 us -> none  [experts(): lax.all_to_all(spread, 'split', split_axis=0, concat_axis=0, tiled=True)]
    ppermute x2 -> x1, starting transfers between devices: 47.8 us -> 43.4 us  [experts(): recv = lax.ppermute(send, 'pair', swap)]
    all_to_all x1, blocking collectives: 21.4 us -> 19 us  [experts(): lax.all_to_all(partial, 'split', split_axis=0, concat_axis=0, tiled=True)]
  transfers between devices with their start and end apart: 4 -> 2, of which waited for: 2 -> 1; matrix products, arithmetic and copies ran while one was open for 1% -> 0% of each run, Pallas kernels for 4% -> 1%
where the time goes in v2:
time: 130 us; the launch traced here: 128 us
  blocking collectives  68.7 us (53%)
  starting transfers between devices  49.4 us (38%)
  Pallas kernels  5.66 us (4%)
  local copies, waits for them, and re-layouts  2.95 us (2%)
    ppermute x1, starting transfers between devices, experts(): recv = lax.ppermute(send, 'pair', swap)  43.4 us
    all_to_all x1, blocking collectives, experts(): lax.all_to_all(spread, 'split', split_axis=0, concat_axis=0, tiled=True)  19.8 us
    all_to_all x1, blocking collectives, experts(): lax.all_to_all(partial, 'split', split_axis=0, concat_axis=0, tiled=True)  19 us
    all_to_all x1, blocking collectives, experts(): lax.all_to_all(returning.reshape(n_expert, rows, width), 'expert', split_...  15.4 us
    all_to_all x1, blocking collectives, experts(): lax.all_to_all(payload, 'expert', split_axis=0, concat_axis=0, tiled=True)  14.6 us
    ppermute x1, starting transfers between devices, experts(): other = lax.ppermute(own, 'pair', swap)  6.04 us
    pallas_call x6, Pallas kernels, call(): pl.pallas_call(kernel, out_shape=outs[0] if single else outs, in_specs=[V...  5.66 us
    unnamed x12, local copies, waits for them, and re-layouts  2.95 us
  transfers between devices with their start and end apart: 2, of which 1 were waited for; matrix products, arithmetic and copies ran while one was open for 0% of the time, Pallas kernels for 1%

profile of v2, /device:TPU:65, one launch (start us, length us, event | category | flops | bytes accessed | tf_op | source)
XLA Modules:
  0.0 128.5 jit_solution(10019198883025469675)
XLA Ops:
  0.0 0.0 copy-start.2
  0.0 0.0 copy-start.3
  0.0 0.0 copy-start.5
  0.0 0.0 copy-start
  0.0 1.7 %copy-done = bf16[1,1792,2,320]{1,3,2,0:T(8,128)(2,1)S(1)} copy-done((bf16[1,1792,2,320]{1,3,2,0:T(8,128)(2,1)S(1)}, bf16[1,1792,2,320]{1,3,2,0:T(8,128)(2,1)}, u32[]{:S(2)}) %copy-start) | copy-done | bytes 2293784
  1.7 0.0 copy-start.1
  1.7 1.3 copy-done.1
  3.0 0.0 copy-start.4
  3.0 3.3 %shard_map.66 = (bf16[4352,256]{1,0:T(8,128)(2,1)S(1)}, bf16[4352,256]{1,0:T(8,128)(2,1)S(1)}) custom-call(s32[1]{0:T(128)} %bitcast.refs_0_.pair_ref, bf16[640,1792]{1,0:T(8,128)(2,1)S(1)} %bitcast.9, bf16[160,3584]{1,0:T(8,128)(2,1)S(1)} %bitcast.10), custom_call_target="tpu_custom_call" | custom-call | tf_op jit(solution)/shard_map/pallas_call | solution.py:116
  6.2 43.4 %collective-permute-start = (bf16[4352,256]{1,0:T(8,128)(2,1)S(1)}, bf16[4352,256]{1,0:T(8,128)(2,1)S(1)}, u32[]{:S(2)}, u32[]{:S(2)}) collective-permute-start(bf16[4352,256]{1,0:T(8,128)(2,1)S(1)} %get-tuple-element.11), channel_id=1, source_target_pairs={{0,1},{1,0},{2,3},{3,2},{4,5},{5,4},{6,7},{7,6},{8,9},{9,8},{10,11... | collective-permute-start | bytes 6684680 | tf_op jit(solution)/shard_map/ppermute | solution.py:151
  49.6 0.0 copy-done.2
  49.6 0.0 copy-done.3
  49.6 0.0 copy-done.5
  49.6 0.0 copy-done.4
  49.6 0.6 shard_map.64
  50.3 14.6 %all_to_all.20 = bf16[16,8,256]{2,1,0:T(8,128)(2,1)S(1)} all-to-all(bf16[16,8,256]{2,1,0:T(8,128)(2,1)S(1)} %shard_map.64), channel_id=1, replica_groups=mesh['groups'=2,'expert'=16,'split'=8,'pair'=2] {'expert'}, dimensions={0} | all-to-all | bytes 131072 | tf_op jit(solution)/shard_map/all_to_all | solution.py:138
  64.9 0.1 shard_map.65
  65.0 19.8 %all_to_all.21.x_ref = bf16[8,224,128]{2,1,0:T(8,128)(2,1)S(1)} all-to-all(bf16[8,224,128]{2,1,0:T(8,128)(2,1)S(1)} %get-tuple-element.9), channel_id=1, replica_groups=mesh['groups'=2,'expert'=16,'split'=8,'pair'=2] {'split'}, dimensions={0} | all-to-all | bytes 917504 | tf_op jit(solution)/shard_map/all_to_all | solution.py:159
  84.8 0.0 collective-permute-done.recv_ref
  84.8 0.8 shard_map.67.own_ref
  85.6 6.0 %collective-permute-start.1 = (bf16[640,128]{1,0:T(8,128)(2,1)S(1)}, bf16[640,128]{1,0:T(8,128)(2,1)S(1)}, u32[]{:S(2)}, u32[]{:S(2)}) collective-permute-start(bf16[640,128]{1,0:T(8,128)(2,1)S(1)} %shard_map.67.own_ref), channel_id=1, source_target_pairs={{0,1},{1,0},{2,3},{3,2},{4,5},{5,4},{6,7},{7,6},{8,9},{9,8},{10,11... | collective-permute-start | bytes 491528 | tf_op jit(solution)/shard_map/ppermute | solution.py:169
  91.7 1.0 collective-permute-done.1.other_ref
  92.7 0.7 shard_map.68
  93.4 19.0 %all_to_all.22.parts_ref = bf16[8,224,128]{2,1,0:T(8,128)(2,1)S(1)} all-to-all(bf16[8,224,128]{2,1,0:T(8,128)(2,1)S(1)} %shard_map.68), channel_id=1, replica_groups=mesh['groups'=2,'expert'=16,'split'=8,'pair'=2] {'split'}, dimensions={0} | all-to-all | bytes 917504 | tf_op jit(solution)/shard_map/all_to_all | solution.py:181
  112.4 0.1 shard_map.69
  112.5 15.4 %all_to_all.23 = bf16[16,8,224]{2,1,0:T(8,128)(2,1)S(1)} all-to-all(bf16[16,8,224]{2,1,0:T(8,128)(2,1)S(1)} %bitcast.12), channel_id=1, replica_groups=mesh['groups'=2,'expert'=16,'split'=8,'pair'=2] {'expert'}, dimensions={0} | all-to-all | bytes 114688 | tf_op jit(solution)/shard_map/all_to_all | solution.py:183
  127.9 0.6 reduce_sum.12
Async XLA Ops:
  0.0 49.6 %copy-start.2 = (bf16[8,224]{1,0:T(8,128)(2,1)S(1)}, bf16[8,224]{1,0:T(8,128)(2,1)}, u32[]{:S(2)}) copy-start(bf16[8,224]{1,0:T(8,128)(2,1)} %tokens_ref.1) | copy-start | bytes 10756
  0.0 49.6 %copy-start.3 = (s32[8,8]{1,0:T(8,128)S(1)}, s32[8,8]{1,0:T(8,128)}, u32[]{:S(2)}) copy-start(s32[8,8]{1,0:T(8,128)} %routes_ref.1) | copy-start | bytes 772
  0.0 49.6 %copy-start.5 = (s32[16]{0:T(128)S(1)}, s32[16]{0:T(128)}, u32[]{:S(2)}) copy-start(s32[16]{0:T(128)} %home_ref.1) | copy-start | bytes 196
  0.0 1.7 %copy-start = (bf16[1,1792,2,320]{1,3,2,0:T(8,128)(2,1)S(1)}, bf16[1,1792,2,320]{1,3,2,0:T(8,128)(2,1)}, u32[]{:S(2)}) copy-start(bf16[1,1792,2,320]{1,3,2,0:T(8,128)(2,1)} %param.10) | copy-start | bytes 6881284
  1.7 1.3 copy-start.1
  3.0 46.7 %copy-start.4 = (f32[8,8]{1,0:T(8,128)S(1)}, f32[8,8]{1,0:T(8,128)}, u32[]{:S(2)}) copy-start(f32[8,8]{1,0:T(8,128)} %combine_ref.1) | copy-start | bytes 772
  6.2 78.6 %collective-permute-start = (bf16[4352,256]{1,0:T(8,128)(2,1)S(1)}, bf16[4352,256]{1,0:T(8,128)(2,1)S(1)}, u32[]{:S(2)}, u32[]{:S(2)}) collective-permute-start(bf16[4352,256]{1,0:T(8,128)(2,1)S(1)} %get-tuple-element.11), channel_id=1, source_target_pairs={{0,1},{1,0},{2,3},{3,2},{4,5},{5,4},{6,7},{7,6},{8,9},{9,8},{10,11... | collective-permute-start | bytes 6684680 | tf_op jit(solution)/shard_map/ppermute | solution.py:151
  85.6 7.1 %collective-permute-start.1 = (bf16[640,128]{1,0:T(8,128)(2,1)S(1)}, bf16[640,128]{1,0:T(8,128)(2,1)S(1)}, u32[]{:S(2)}, u32[]{:S(2)}) collective-permute-start(bf16[640,128]{1,0:T(8,128)(2,1)S(1)} %shard_map.67.own_ref), channel_id=1, source_target_pairs={{0,1},{1,0},{2,3},{3,2},{4,5},{5,4},{6,7},{7,6},{8,9},{9,8},{10,11... | collective-permute-start | bytes 491528 | tf_op jit(solution)/shard_map/ppermute | solution.py:169

commit v3 on v2

v3 whole, which is shorter than its diff:
```python
import jax
import jax.numpy as jnp
from jax import lax
from jax.experimental import pallas as pl
from jax.experimental.pallas import tpu as pltpu
from jax.sharding import PartitionSpec as P

VMEM = pl.BlockSpec(memory_space=pltpu.VMEM)
LANES = 128
GRANT = 16 << 20
BF16 = jnp.bfloat16


def padded(value, lanes):
    rows, width = value.shape
    if width == lanes:
        return value
    return jnp.concatenate([value, jnp.zeros((rows, lanes - width), value.dtype)], axis=1)


def fetched(sources, targets, semaphores):
    copies = [
        pltpu.make_async_copy(source, target, semaphores.at[i]) for i, (source, target) in enumerate(zip(sources, targets))
    ]
    for copy in copies:
        copy.start()
    for copy in copies:
        copy.wait()


def dispatch_kernel(home_hbm, tokens_hbm, routes_hbm, combine_hbm, out_ref, home_ref, tokens_ref, routes_ref, combine_ref, semaphores):
    fetched(
        (home_hbm, tokens_hbm, routes_hbm, combine_hbm), (home_ref, tokens_ref, routes_ref, combine_ref), semaphores
    )
    slots, rows, lanes = out_ref.shape
    width = tokens_ref.shape[1]
    routes = routes_ref[...]
    combine = combine_ref[...]
    slot = jnp.zeros_like(routes)
    for expert in range(slots):
        slot = jnp.where(routes == expert, home_ref[expert], slot)
    tokens = padded(tokens_ref[...].astype(jnp.float32), lanes)
    lane = lax.broadcasted_iota(jnp.int32, (rows, lanes), 1)
    for s in range(slots):
        weight = jnp.sum(jnp.where(slot == s, combine, 0.0), axis=1, keepdims=True)
        high = weight.astype(jnp.bfloat16).astype(jnp.float32)
        value = jnp.where(lane == width, high, jnp.where(lane == width + 1, weight - high, tokens))
        out_ref[s] = value.astype(jnp.bfloat16)


def arrange_kernel(pair_ref, down_hbm, keep_ref, send_ref, down_ref, semaphores):
    fetched((down_hbm,), (down_ref,), semaphores)
    even = pair_ref[0] == 0
    width = keep_ref.shape[2]
    for i in range(keep_ref.shape[0]):
        first = down_ref[:, 2 * i * width : (2 * i + 1) * width]
        second = down_ref[:, (2 * i + 1) * width : (2 * i + 2) * width]
        keep_ref[i] = jnp.where(even, first, second)
        send_ref[i] = jnp.where(even, second, first)


def turn_kernel(arrived_ref, x_ref, weight_ref):
    width = x_ref.shape[0]
    turned = arrived_ref[...].astype(jnp.float32).T
    x_ref[...] = turned[:width].astype(x_ref.dtype)
    weight_ref[...] = turned[width : width + 1] + turned[width + 1 : width + 2]


def expert_kernel(pair_ref, x_ref, own_ref, other_ref, weight_ref, keep_ref, recv_ref, out_ref):
    pair = pair_ref[0]
    half = own_ref.shape[1]

    def part(ref, index):
        return jnp.dot(ref[...], x_ref[pl.ds(index * half, half), :], preferred_element_type=jnp.float32)

    before = part(own_ref, pair) + part(other_ref, 1 - pair)
    units = before.shape[0] // 2
    gate, up = before[:units], before[units:]
    hidden = gate / (1.0 + jnp.exp(-gate)) * up * weight_ref[...]
    even = pair == 0
    depth = units // 2
    low, high = hidden[:depth].T.astype(BF16), hidden[depth:].T.astype(BF16)
    own = jnp.where(even, low, high)
    other = jnp.where(even, high, low)
    for i in range(out_ref.shape[0]):
        total = jnp.dot(own, keep_ref[i], preferred_element_type=jnp.float32)
        total = total + jnp.dot(other, recv_ref[i], preferred_element_type=jnp.float32)
        out_ref[i] = total.T.astype(out_ref.dtype)


def gather_kernel(parts_ref, out_ref):
    total = parts_ref[0].astype(jnp.float32)
    for i in range(1, parts_ref.shape[0]):
        total = total + parts_ref[i].astype(jnp.float32)
    out_ref[...] = total.T.astype(out_ref.dtype)


def call(kernel, outs, spaces, operands, scratch=()):
    outs = [pltpu.VMEM(shape, dtype) for shape, dtype in outs]
    operands = [
        operand if space is pltpu.SMEM else pltpu.with_memory_space_constraint(operand, space)
        for operand, space in zip(operands, spaces)
    ]
    single = len(outs) == 1
    return pl.pallas_call(
        kernel,
        out_shape=outs[0] if single else outs,
        in_specs=[pl.BlockSpec(memory_space=space) for space in spaces],
        out_specs=VMEM if single else [VMEM] * len(outs),
        scratch_shapes=list(scratch),
        compiler_params=pltpu.CompilerParams(vmem_limit_bytes=GRANT),
    )(*operands)


def experts(tokens, routes, combine, home, gate_up, down):
    n_expert, n_split, _ = (lax.axis_size(name) for name in ("expert", "split", "pair"))
    rows, width = tokens.shape
    lanes = -(-(width + 2) // LANES) * LANES
    features = gate_up.shape[1]
    units = gate_up.shape[3]
    total_rows = n_expert * rows
    pair = lax.axis_index("pair").astype(jnp.int32).reshape(1)
    swap = [(0, 1), (1, 0)]
    inner, outer, scalars = pltpu.VMEM, pltpu.HBM, pltpu.SMEM

    payload = call(
        dispatch_kernel,
        [((n_expert, rows, lanes), BF16)],
        [outer] * 4,
        [home, tokens, routes, combine],
        [
            pltpu.SMEM(home.shape, home.dtype),
            pltpu.VMEM(tokens.shape, tokens.dtype),
            pltpu.VMEM(routes.shape, routes.dtype),
            pltpu.VMEM(combine.shape, combine.dtype),
            pltpu.SemaphoreType.DMA((4,)),
        ],
    )
    arrived = lax.all_to_all(payload, "expert", split_axis=0, concat_axis=0, tiled=True)

    up_own = jnp.transpose(gate_up[0], (1, 2, 0)).reshape(2 * units, features)
    up_other = lax.ppermute(up_own, "pair", swap)
    keep, send = call(
        arrange_kernel,
        [((n_split, down.shape[1], width), BF16)] * 2,
        [scalars, outer],
        [pair, down[0]],
        [pltpu.VMEM(down.shape[1:], down.dtype), pltpu.SemaphoreType.DMA((1,))],
    )
    recv = lax.ppermute(send, "pair", swap)

    turned, weight = call(
        turn_kernel,
        [((width, total_rows), BF16), ((1, total_rows), jnp.float32)],
        [inner],
        [arrived.reshape(total_rows, lanes)],
    )
    gathered = lax.all_gather(turned, ("split", "pair"), axis=0, tiled=True)
    partial = call(
        expert_kernel,
        [((n_split, width, total_rows), BF16)],
        [scalars] + [inner] * 6,
        [pair, gathered, up_own, up_other, weight, keep, recv],
    )
    parts = lax.all_to_all(partial, "split", split_axis=0, concat_axis=0, tiled=True)
    returning = call(gather_kernel, [((total_rows, width), BF16)], [inner], [parts])
    results = lax.all_to_all(
        returning.reshape(n_expert, rows, width), "expert", split_axis=0, concat_axis=0, tiled=True
    )
    return results.astype(jnp.float32).sum(axis=0).astype(BF16)


def solution(mesh):
    placed = (
        P(("groups", "expert"), ("split", "pair")),
        P(("groups", "expert"), None),
        P(("groups", "expert"), None),
        P(),
        P("expert", "pair", None, "split"),
        P("expert", ("split", "pair"), None),
    )
    return jax.shard_map(
        experts,
        mesh=mesh,
        in_specs=placed,
        out_specs=P(("groups", "expert"), ("split", "pair")),
        check_vma=False,
    )
```

time: 130 us -> 124 us (0.954)
  blocking collectives: 68.7 us -> 57.8 us
  waiting for transfers between devices: 1.01 us -> 5.59 us
  Pallas kernels: 5.66 us -> 9.6 us
  local copies, waits for them, and re-layouts: 2.95 us -> 0.01 us
    ppermute x1, starting transfers between devices: 43.4 us -> 1.95 us  [experts(): recv = lax.ppermute(send, 'pair', swap)]
    ppermute x1, starting transfers between devices: 6.04 us -> 43.5 us  [experts(): up_other = lax.ppermute(up_own, 'pair', swap)]
    all_to_all x2 -> x0, blocking collectives: 34.4 us -> none  [the longest x1 19.8 us: experts(): lax.all_to_all(spread, 'split', split_axis=0, concat_axis=0, tiled=True)]
    all_gather x0 -> x1, blocking collectives: none -> 22.1 us  [experts(): gathered = lax.all_gather(turned, ('split', 'pair'), axis=0, tiled=True)]
    all_to_all x0 -> x1, waiting for transfers between devices: none -> 5.59 us  [experts(): lax.all_to_all(payload, 'expert', split_axis=0, concat_axis=0, tiled=True)]
    all_to_all x0 -> x1, starting transfers between devices: none -> 3.95 us  [experts(): lax.all_to_all(payload, 'expert', split_axis=0, concat_axis=0, tiled=True)]
    pallas_call x6 -> x5, Pallas kernels: 5.66 us -> 9.6 us  [call(): pl.pallas_call(kernel, out_shape=outs[0] if single else outs, in_specs=[p...]
    unnamed x12 -> x2, local copies, waits for them, and re-layouts: 2.95 us -> 0.01 us
  transfers between devices with their start and end apart: 2 -> 3, of which waited for: 1 -> 1; matrix products, arithmetic and copies ran while one was open for 0% -> 0% of each run, Pallas kernels for 1% -> 4%
where the time goes in v3:
time: 124 us; the launch traced here: 123 us
  blocking collectives  57.8 us (47%)
  starting transfers between devices  49.4 us (40%)
  Pallas kernels  9.6 us (8%)
  waiting for transfers between devices  5.59 us (5%)
    ppermute x1, starting transfers between devices, experts(): up_other = lax.ppermute(up_own, 'pair', swap)  43.5 us
    all_gather x1, blocking collectives, experts(): gathered = lax.all_gather(turned, ('split', 'pair'), axis=0, tiled=True)  22.1 us
    all_to_all x1, blocking collectives, experts(): lax.all_to_all(partial, 'split', split_axis=0, concat_axis=0, tiled=True)  20.2 us
    all_to_all x1, blocking collectives, experts(): lax.all_to_all(returning.reshape(n_expert, rows, width), 'expert', split_...  15.5 us
    pallas_call x5, Pallas kernels, call(): pl.pallas_call(kernel, out_shape=outs[0] if single else outs, in_specs=[p...  9.6 us
    all_to_all x1, waiting for transfers between devices, experts(): lax.all_to_all(payload, 'expert', split_axis=0, concat_axis=0, tiled=True)  5.59 us
    all_to_all x1, starting transfers between devices, experts(): lax.all_to_all(payload, 'expert', split_axis=0, concat_axis=0, tiled=True)  3.95 us
  transfers between devices with their start and end apart: 3, of which 1 were waited for; matrix products, arithmetic and copies ran while one was open for 0% of the time, Pallas kernels for 4%

profile of v3, /device:TPU:65, one launch (start us, length us, event | category | flops | bytes accessed | tf_op | source)
XLA Modules:
  0.0 123.1 jit_solution(15811327573062011253)
XLA Ops:
  0.0 0.0 copy-start
  0.0 43.5 %collective-permute-start = (bf16[640,1792]{1,0:T(8,128)(2,1)}, bf16[640,1792]{1,0:T(8,128)(2,1)}, u32[]{:S(2)}, u32[]{:S(2)}) collective-permute-start(bf16[640,1792]{1,0:T(8,128)(2,1)} %bitcast.9), channel_id=1, source_target_pairs={{0,1},{1,0},{2,3},{3,2},{4,5},{5,4},{6,7},{7,6},{8,9},{9,8},{10,11... | collective-permute-start | bytes 6881288 | tf_op jit(solution)/shard_map/ppermute | solution.py:142
  43.5 1.5 %shard_map.64 = bf16[16,8,256]{2,1,0:T(8,128)(2,1)} custom-call(s32[16]{0:T(128)} %home_hbm.1, bf16[8,224]{1,0:T(8,128)(2,1)} %tokens_hbm.1, s32[8,8]{1,0:T(8,128)} %routes_hbm.1, f32[8,8]{1,0:T(8,128)} %combine_hbm.1), custom_call_target="tpu_custom_call" | custom-call | tf_op jit(solution)/shard_map/pallas_call | solution.py:105
  45.0 3.9 %all-to-all-start = ((bf16[16,8,256]{2,1,0:T(8,128)(2,1)}), bf16[16,8,256]{2,1,0:T(8,128)(2,1)S(1)}, u32[]{:S(2)}, u32[]{:S(2)}) async-start(bf16[16,8,256]{2,1,0:T(8,128)(2,1)} %shard_map.64), calls=%async_computation | async-start | bytes 131072 | tf_op jit(solution)/shard_map/all_to_all | solution.py:139
  49.0 3.7 %shard_map.66 = (bf16[8,160,224]{2,1,0:T(8,128)(2,1)S(1)}, bf16[8,160,224]{2,1,0:T(8,128)(2,1)}) custom-call(s32[1]{0:T(128)} %bitcast.pair_ref, bf16[160,3584]{1,0:T(8,128)(2,1)} %bitcast.13), custom_call_target="tpu_custom_call" | custom-call | tf_op jit(solution)/shard_map/pallas_call | solution.py:105
  52.6 2.0 %collective-permute-start.1 = (bf16[8,160,224]{2,1,0:T(8,128)(2,1)}, bf16[8,160,224]{2,1,0:T(8,128)(2,1)}, u32[]{:S(2)}, u32[]{:S(2)}) collective-permute-start(bf16[8,160,224]{2,1,0:T(8,128)(2,1)} %get-tuple-element.12), channel_id=1, source_target_pairs={{0,1},{1,0},{2,3},{3,2},{4,5},{5,4},{6,7},{7,6},{8,9},{9,8},{10,11... | collective-permute-start | bytes 1720328 | tf_op jit(solution)/shard_map/ppermute | solution.py:150
  54.6 5.6 %all-to-all-done = bf16[16,8,256]{2,1,0:T(8,128)(2,1)S(1)} async-done(((bf16[16,8,256]{2,1,0:T(8,128)(2,1)}), bf16[16,8,256]{2,1,0:T(8,128)(2,1)S(1)}, u32[]{:S(2)}, u32[]{:S(2)}) %all-to-all-start) | async-done | bytes 65568 | tf_op jit(solution)/shard_map/all_to_all | solution.py:139
  60.2 0.1 shard_map.65
  60.3 22.1 %all_gather.3.x_ref = bf16[3584,128]{1,0:T(8,128)(2,1)S(1)} all-gather(bf16[224,128]{1,0:T(8,128)(2,1)S(1)} %get-tuple-element.9), channel_id=1, replica_groups=mesh['groups'=2,'expert'=16,'split'=8,'pair'=2] {'split','pair'}, dimensions={0}, use_global_device_ids=true | all-gather | bytes 974848 | tf_op jit(solution)/shard_map/all_gather | solution.py:158
  82.4 0.0 collective-permute-done.1.recv_ref
  82.4 0.0 collective-permute-done.other_ref
  82.4 0.0 copy-done
  82.4 4.2 %shard_map.67 = bf16[8,224,128]{2,1,0:T(8,128)(2,1)S(1)} custom-call(s32[1]{0:T(128)} %bitcast.pair_ref, bf16[3584,128]{1,0:T(8,128)(2,1)S(1)} %all_gather.3.x_ref, bf16[640,1792]{1,0:T(8,128)(2,1)S(1)} %bitcast.10, bf16[640,1792]{1,0:T(8,128)(2,1)} %collective-permute-done.other_ref, f32[1,128]{1,0:T(1,128)S(1)} %get-tuple-element.10.weight_ref, ...), custom_call_target="tpu_custom_call" | custom-call | tf_op jit(solution)/shard_map/pallas_call | solution.py:105
  86.6 20.2 %all_to_all.15.parts_ref = bf16[8,224,128]{2,1,0:T(8,128)(2,1)S(1)} all-to-all(bf16[8,224,128]{2,1,0:T(8,128)(2,1)S(1)} %shard_map.67), channel_id=1, replica_groups=mesh['groups'=2,'expert'=16,'split'=8,'pair'=2] {'split'}, dimensions={0} | all-to-all | bytes 917504 | tf_op jit(solution)/shard_map/all_to_all | solution.py:165
  106.8 0.1 shard_map.68
  107.0 15.5 %all_to_all.16 = bf16[16,8,224]{2,1,0:T(8,128)(2,1)S(1)} all-to-all(bf16[16,8,224]{2,1,0:T(8,128)(2,1)S(1)} %bitcast.12), channel_id=1, replica_groups=mesh['groups'=2,'expert'=16,'split'=8,'pair'=2] {'expert'}, dimensions={0} | all-to-all | bytes 114688 | tf_op jit(solution)/shard_map/all_to_all | solution.py:167
  122.5 0.6 reduce_sum.12
Async XLA Ops:
  0.0 82.4 %copy-start = (bf16[1,1792,2,320]{1,3,2,0:T(8,128)(2,1)S(1)}, bf16[1,1792,2,320]{1,3,2,0:T(8,128)(2,1)}, u32[]{:S(2)}) copy-start(bf16[1,1792,2,320]{1,3,2,0:T(8,128)(2,1)} %param.10) | copy-start | bytes 6881284
  0.0 82.4 %collective-permute-start = (bf16[640,1792]{1,0:T(8,128)(2,1)}, bf16[640,1792]{1,0:T(8,128)(2,1)}, u32[]{:S(2)}, u32[]{:S(2)}) collective-permute-start(bf16[640,1792]{1,0:T(8,128)(2,1)} %bitcast.9), channel_id=1, source_target_pairs={{0,1},{1,0},{2,3},{3,2},{4,5},{5,4},{6,7},{7,6},{8,9},{9,8},{10,11... | collective-permute-start | bytes 6881288 | tf_op jit(solution)/shard_map/ppermute | solution.py:142
  45.0 15.2 %all-to-all-start = ((bf16[16,8,256]{2,1,0:T(8,128)(2,1)}), bf16[16,8,256]{2,1,0:T(8,128)(2,1)S(1)}, u32[]{:S(2)}, u32[]{:S(2)}) async-start(bf16[16,8,256]{2,1,0:T(8,128)(2,1)} %shard_map.64), calls=%async_computation | async-start | bytes 131072 | tf_op jit(solution)/shard_map/all_to_all | solution.py:139
  52.6 29.7 %collective-permute-start.1 = (bf16[8,160,224]{2,1,0:T(8,128)(2,1)}, bf16[8,160,224]{2,1,0:T(8,128)(2,1)}, u32[]{:S(2)}, u32[]{:S(2)}) collective-permute-start(bf16[8,160,224]{2,1,0:T(8,128)(2,1)} %get-tuple-element.12), channel_id=1, source_target_pairs={{0,1},{1,0},{2,3},{3,2},{4,5},{5,4},{6,7},{7,6},{8,9},{9,8},{10,11... | collective-permute-start | bytes 1720328 | tf_op jit(solution)/shard_map/ppermute | solution.py:150

commit v4 on v3

--- a/solution.py
+++ b/solution.py
@@ -48,17 +48,6 @@
         out_ref[s] = value.astype(jnp.bfloat16)
 
 
-def arrange_kernel(pair_ref, down_hbm, keep_ref, send_ref, down_ref, semaphores):
-    fetched((down_hbm,), (down_ref,), semaphores)
-    even = pair_ref[0] == 0
-    width = keep_ref.shape[2]
-    for i in range(keep_ref.shape[0]):
-        first = down_ref[:, 2 * i * width : (2 * i + 1) * width]
-        second = down_ref[:, (2 * i + 1) * width : (2 * i + 2) * width]
-        keep_ref[i] = jnp.where(even, first, second)
-        send_ref[i] = jnp.where(even, second, first)
-
-
 def turn_kernel(arrived_ref, x_ref, weight_ref):
     width = x_ref.shape[0]
     turned = arrived_ref[...].astype(jnp.float32).T
@@ -66,14 +55,22 @@
     weight_ref[...] = turned[width : width + 1] + turned[width + 1 : width + 2]
 
 
-def expert_kernel(pair_ref, x_ref, own_ref, other_ref, weight_ref, keep_ref, recv_ref, out_ref):
+def expert_kernel(
+    pair_ref, x_ref, up_hbm, up_other, weight_ref, down_hbm, down_other, out_ref, up_own, down_own, semaphores
+):
+    up_copy = pltpu.make_async_copy(up_hbm, up_own, semaphores.at[0])
+    down_copy = pltpu.make_async_copy(down_hbm, down_own, semaphores.at[1])
+    up_copy.start()
+    down_copy.start()
     pair = pair_ref[0]
-    half = own_ref.shape[1]
+    half = up_own.shape[1]
 
     def part(ref, index):
         return jnp.dot(ref[...], x_ref[pl.ds(index * half, half), :], preferred_element_type=jnp.float32)
 
-    before = part(own_ref, pair) + part(other_ref, 1 - pair)
+    before = part(up_other, 1 - pair)
+    up_copy.wait()
+    before = before + part(up_own, pair)
     units = before.shape[0] // 2
     gate, up = before[:units], before[units:]
     hidden = gate / (1.0 + jnp.exp(-gate)) * up * weight_ref[...]
@@ -82,10 +79,20 @@
     low, high = hidden[:depth].T.astype(BF16), hidden[depth:].T.astype(BF16)
     own = jnp.where(even, low, high)
     other = jnp.where(even, high, low)
-    for i in range(out_ref.shape[0]):
-        total = jnp.dot(own, keep_ref[i], preferred_element_type=jnp.float32)
-        total = total + jnp.dot(other, recv_ref[i], preferred_element_type=jnp.float32)
-        out_ref[i] = total.T.astype(out_ref.dtype)
+    blocks, width, _ = out_ref.shape
+    down_copy.wait()
+
+    def blocks_of(parity):
+        for i in range(blocks):
+            start = (2 * i + parity) * width
+            first = start // LANES * LANES
+            last = -(-(start + width) // LANES) * LANES
+            total = jnp.dot(own, down_own[:, first:last], preferred_element_type=jnp.float32)
+            total = total + jnp.dot(other, down_other[:, first:last], preferred_element_type=jnp.float32)
+            out_ref[i] = total.T[start - first : start - first + width].astype(out_ref.dtype)
+
+    pl.when(even)(lambda: blocks_of(0))
+    pl.when(jnp.logical_not(even))(lambda: blocks_of(1))
 
 
 def gather_kernel(parts_ref, out_ref):
@@ -140,14 +147,7 @@
 
     up_own = jnp.transpose(gate_up[0], (1, 2, 0)).reshape(2 * units, features)
     up_other = lax.ppermute(up_own, "pair", swap)
-    keep, send = call(
-        arrange_kernel,
-        [((n_split, down.shape[1], width), BF16)] * 2,
-        [scalars, outer],
-        [pair, down[0]],
-        [pltpu.VMEM(down.shape[1:], down.dtype), pltpu.SemaphoreType.DMA((1,))],
-    )
-    recv = lax.ppermute(send, "pair", swap)
+    down_other = lax.ppermute(down[0], "pair", swap)
 
     turned, weight = call(
         turn_kernel,
@@ -159,8 +159,13 @@
     partial = call(
         expert_kernel,
         [((n_split, width, total_rows), BF16)],
-        [scalars] + [inner] * 6,
-        [pair, gathered, up_own, up_other, weight, keep, recv],
+        [scalars, inner, outer, inner, inner, outer, inner],
+        [pair, gathered, up_own, up_other, weight, down[0], down_other],
+        [
+            pltpu.VMEM(up_own.shape, up_own.dtype),
+            pltpu.VMEM(down.shape[1:], down.dtype),
+            pltpu.SemaphoreType.DMA((2,)),
+        ],
     )
     parts = lax.all_to_all(partial, "split", split_axis=0, concat_axis=0, tiled=True)
     returning = call(gather_kernel, [((total_rows, width), BF16)], [inner], [parts])

time: 124 us -> 124 us (level)
  waiting for transfers between devices: 5.59 us -> 11.2 us
  Pallas kernels: 9.6 us -> 4.87 us
    all_to_all x1, waiting for transfers between devices: 5.59 us -> 11.2 us  [experts(): lax.all_to_all(payload, 'expert', split_axis=0, concat_axis=0, tiled=True)]
    pallas_call x5 -> x4, Pallas kernels: 9.6 us -> 4.87 us  [call(): pl.pallas_call(kernel, out_shape=outs[0] if single else outs, in_specs=[p...]
  transfers between devices with their start and end apart: 3 -> 3, of which waited for: 1 -> 1; matrix products, arithmetic and copies ran while one was open for 0% -> 0% of each run, Pallas kernels for 4% -> 1%
where the time goes in v4:
time: 124 us; the launch traced here: 123 us
  blocking collectives  56.8 us (46%)
  starting transfers between devices  49.2 us (40%)
  waiting for transfers between devices  11.2 us (9%)
  Pallas kernels  4.87 us (4%)
    ppermute x1, starting transfers between devices, experts(): up_other = lax.ppermute(up_own, 'pair', swap)  43.4 us
    all_gather x1, blocking collectives, experts(): gathered = lax.all_gather(turned, ('split', 'pair'), axis=0, tiled=True)  22.2 us
    all_to_all x1, blocking collectives, experts(): lax.all_to_all(partial, 'split', split_axis=0, concat_axis=0, tiled=True)  20.2 us
    all_to_all x1, blocking collectives, experts(): lax.all_to_all(returning.reshape(n_expert, rows, width), 'expert', split_...  14.3 us
    all_to_all x1, waiting for transfers between devices, experts(): lax.all_to_all(payload, 'expert', split_axis=0, concat_axis=0, tiled=True)  11.2 us
    pallas_call x4, Pallas kernels, call(): pl.pallas_call(kernel, out_shape=outs[0] if single else outs, in_specs=[p...  4.87 us
    all_to_all x1, starting transfers between devices, experts(): lax.all_to_all(payload, 'expert', split_axis=0, concat_axis=0, tiled=True)  3.93 us
  transfers between devices with their start and end apart: 3, of which 1 were waited for; matrix products, arithmetic and copies ran while one was open for 0% of the time, Pallas kernels for 1%

profile of v4, /device:TPU:65, one launch (start us, length us, event | category | flops | bytes accessed | tf_op | source)
XLA Modules:
  0.0 123.5 jit_solution(2159854220655124179)
XLA Ops:
  0.0 43.4 %collective-permute-start = (bf16[640,1792]{1,0:T(8,128)(2,1)}, bf16[640,1792]{1,0:T(8,128)(2,1)S(1)}, u32[]{:S(2)}, u32[]{:S(2)}) collective-permute-start(bf16[640,1792]{1,0:T(8,128)(2,1)} %bitcast.11), channel_id=1, source_target_pairs={{0,1},{1,0},{2,3},{3,2},{4,5},{5,4},{6,7},{7,6},{8,9},{9,8},{10,11... | collective-permute-start | bytes 6881288 | tf_op jit(solution)/shard_map/ppermute | solution.py:149
  43.4 2.0 %collective-permute-start.1 = (bf16[160,3584]{1,0:T(8,128)(2,1)}, bf16[160,3584]{1,0:T(8,128)(2,1)S(1)}, u32[]{:S(2)}, u32[]{:S(2)}) collective-permute-start(bf16[160,3584]{1,0:T(8,128)(2,1)} %bitcast.13), channel_id=1, source_target_pairs={{0,1},{1,0},{2,3},{3,2},{4,5},{5,4},{6,7},{7,6},{8,9},{9,8},{10,11... | collective-permute-start | bytes 3440648 | tf_op jit(solution)/shard_map/ppermute | solution.py:150
  45.3 0.9 shard_map.64
  46.2 0.0 copy-start
  46.2 0.6 copy-done
  46.8 3.9 %all-to-all-start = ((bf16[16,8,256]{2,1,0:T(8,128)(2,1)}), bf16[16,8,256]{2,1,0:T(8,128)(2,1)S(1)}, u32[]{:S(2)}, u32[]{:S(2)}) async-start(bf16[16,8,256]{2,1,0:T(8,128)(2,1)} %copy-done), calls=%async_computation | async-start | bytes 131072 | tf_op jit(solution)/shard_map/all_to_all | solution.py:146
  50.8 11.2 %all-to-all-done = bf16[16,8,256]{2,1,0:T(8,128)(2,1)S(1)} async-done(((bf16[16,8,256]{2,1,0:T(8,128)(2,1)}), bf16[16,8,256]{2,1,0:T(8,128)(2,1)S(1)}, u32[]{:S(2)}, u32[]{:S(2)}) %all-to-all-start) | async-done | bytes 65568 | tf_op jit(solution)/shard_map/all_to_all | solution.py:146
  62.0 0.1 shard_map.65
  62.1 22.2 %all_gather.3.x_ref = bf16[3584,128]{1,0:T(8,128)(2,1)S(1)} all-gather(bf16[224,128]{1,0:T(8,128)(2,1)S(1)} %get-tuple-element.7), channel_id=1, replica_groups=mesh['groups'=2,'expert'=16,'split'=8,'pair'=2] {'split','pair'}, dimensions={0}, use_global_device_ids=true | all-gather | bytes 974848 | tf_op jit(solution)/shard_map/all_gather | solution.py:158
  84.3 0.0 collective-permute-done.1.down_other
  84.3 0.0 collective-permute-done.up_other
  84.4 3.8 %shard_map.66 = bf16[8,224,128]{2,1,0:T(8,128)(2,1)S(1)} custom-call(s32[1]{0:T(128)} %bitcast.pair_ref, bf16[3584,128]{1,0:T(8,128)(2,1)S(1)} %all_gather.3.x_ref, bf16[640,1792]{1,0:T(8,128)(2,1)} %bitcast.12, bf16[640,1792]{1,0:T(8,128)(2,1)S(1)} %collective-permute-done.up_other, f32[1,128]{1,0:T(1,128)S(1)} %get-tuple-element.8.weight_ref, ...), custom_call_target="tpu_custom_call" | custom-call | tf_op jit(solution)/shard_map/pallas_call | solution.py:112
  88.1 20.2 %all_to_all.15.parts_ref = bf16[8,224,128]{2,1,0:T(8,128)(2,1)S(1)} all-to-all(bf16[8,224,128]{2,1,0:T(8,128)(2,1)S(1)} %shard_map.66), channel_id=1, replica_groups=mesh['groups'=2,'expert'=16,'split'=8,'pair'=2] {'split'}, dimensions={0} | all-to-all | bytes 917504 | tf_op jit(solution)/shard_map/all_to_all | solution.py:170
  108.4 0.1 shard_map.67
  108.5 14.3 %all_to_all.16 = bf16[16,8,224]{2,1,0:T(8,128)(2,1)S(1)} all-to-all(bf16[16,8,224]{2,1,0:T(8,128)(2,1)S(1)} %bitcast.10), channel_id=1, replica_groups=mesh['groups'=2,'expert'=16,'split'=8,'pair'=2] {'expert'}, dimensions={0} | all-to-all | bytes 114688 | tf_op jit(solution)/shard_map/all_to_all | solution.py:172
  122.9 0.6 reduce_sum.12
Async XLA Ops:
  0.0 84.4 %collective-permute-start = (bf16[640,1792]{1,0:T(8,128)(2,1)}, bf16[640,1792]{1,0:T(8,128)(2,1)S(1)}, u32[]{:S(2)}, u32[]{:S(2)}) collective-permute-start(bf16[640,1792]{1,0:T(8,128)(2,1)} %bitcast.11), channel_id=1, source_target_pairs={{0,1},{1,0},{2,3},{3,2},{4,5},{5,4},{6,7},{7,6},{8,9},{9,8},{10,11... | collective-permute-start | bytes 6881288 | tf_op jit(solution)/shard_map/ppermute | solution.py:149
  43.4 41.0 %collective-permute-start.1 = (bf16[160,3584]{1,0:T(8,128)(2,1)}, bf16[160,3584]{1,0:T(8,128)(2,1)S(1)}, u32[]{:S(2)}, u32[]{:S(2)}) collective-permute-start(bf16[160,3584]{1,0:T(8,128)(2,1)} %bitcast.13), channel_id=1, source_target_pairs={{0,1},{1,0},{2,3},{3,2},{4,5},{5,4},{6,7},{7,6},{8,9},{9,8},{10,11... | collective-permute-start | bytes 3440648 | tf_op jit(solution)/shard_map/ppermute | solution.py:150
  46.2 0.6 copy-start
  46.8 15.2 %all-to-all-start = ((bf16[16,8,256]{2,1,0:T(8,128)(2,1)}), bf16[16,8,256]{2,1,0:T(8,128)(2,1)S(1)}, u32[]{:S(2)}, u32[]{:S(2)}) async-start(bf16[16,8,256]{2,1,0:T(8,128)(2,1)} %copy-done), calls=%async_computation | async-start | bytes 131072 | tf_op jit(solution)/shard_map/all_to_all | solution.py:146

commit v5 on v4

--- a/solution.py
+++ b/solution.py
@@ -56,21 +56,43 @@
 
 
 def expert_kernel(
-    pair_ref, x_ref, up_hbm, up_other, weight_ref, down_hbm, down_other, out_ref, up_own, down_own, semaphores
+    pair_ref,
+    x_ref,
+    up_hbm,
+    up_other,
+    weight_ref,
+    down_hbm,
+    down_other,
+    out_ref,
+    up_own,
+    down_own,
+    before_ref,
+    up_semaphores,
+    down_semaphore,
 ):
-    up_copy = pltpu.make_async_copy(up_hbm, up_own, semaphores.at[0])
-    down_copy = pltpu.make_async_copy(down_hbm, down_own, semaphores.at[1])
-    up_copy.start()
-    down_copy.start()
+    rows, half = up_own.shape
+    chunks = up_semaphores.shape[0]
+    depth = half // chunks
+    columns = [slice(i * depth, (i + 1) * depth) for i in range(chunks)]
+    up_copies = [
+        pltpu.make_async_copy(up_hbm.at[:, part], up_own.at[:, part], up_semaphores.at[i])
+        for i, part in enumerate(columns)
+    ]
+    down_copy = pltpu.make_async_copy(down_hbm, down_own, down_semaphore)
+    for copy in (*up_copies, down_copy):
+        copy.start()
     pair = pair_ref[0]
-    half = up_own.shape[1]
-
-    def part(ref, index):
-        return jnp.dot(ref[...], x_ref[pl.ds(index * half, half), :], preferred_element_type=jnp.float32)
-
-    before = part(up_other, 1 - pair)
-    up_copy.wait()
-    before = before + part(up_own, pair)
+    bands = (slice(0, rows // 2), slice(rows // 2, rows))
+    x = x_ref[pl.ds((1 - pair) * half, half), :]
+    for band in bands:
+        before_ref[band] = jnp.dot(up_other[band], x, preferred_element_type=jnp.float32)
+    for i, part in enumerate(columns):
+        up_copies[i].wait()
+        x = x_ref[pl.ds(pair * half + i * depth, depth), :]
+        for band in bands:
+            product = jnp.dot(up_own[band, part], x, preferred_element_type=jnp.float32)
+            before_ref[band] = before_ref[band] + product
+    before = before_ref[...]
     units = before.shape[0] // 2
     gate, up = before[:units], before[units:]
     hidden = gate / (1.0 + jnp.exp(-gate)) * up * weight_ref[...]
@@ -164,7 +186,9 @@
         [
             pltpu.VMEM(up_own.shape, up_own.dtype),
             pltpu.VMEM(down.shape[1:], down.dtype),
-            pltpu.SemaphoreType.DMA((2,)),
+            pltpu.VMEM((2 * units, total_rows), jnp.float32),
+            pltpu.SemaphoreType.DMA((features // (2 * LANES),)),
+            pltpu.SemaphoreType.DMA,
         ],
     )
     parts = lax.all_to_all(partial, "split", split_axis=0, concat_axis=0, tiled=True)

time: 124 us -> 124 us (level)
  no operation moved by 1% of the time
where the time goes in v5:
time: 124 us; the launch traced here: 123 us
  blocking collectives  56.8 us (46%)
  starting transfers between devices  49.2 us (40%)
  waiting for transfers between devices  11.2 us (9%)
  Pallas kernels  4.4 us (4%)
    ppermute x1, starting transfers between devices, experts(): up_other = lax.ppermute(up_own, 'pair', swap)  43.4 us
    all_gather x1, blocking collectives, experts(): gathered = lax.all_gather(turned, ('split', 'pair'), axis=0, tiled=True)  22.2 us
    all_to_all x1, blocking collectives, experts(): lax.all_to_all(partial, 'split', split_axis=0, concat_axis=0, tiled=True)  20.2 us
    all_to_all x1, blocking collectives, experts(): lax.all_to_all(returning.reshape(n_expert, rows, width), 'expert', split_...  14.3 us
    all_to_all x1, waiting for transfers between devices, experts(): lax.all_to_all(payload, 'expert', split_axis=0, concat_axis=0, tiled=True)  11.2 us
    pallas_call x4, Pallas kernels, call(): pl.pallas_call(kernel, out_shape=outs[0] if single else outs, in_specs=[p...  4.4 us
    all_to_all x1, starting transfers between devices, experts(): lax.all_to_all(payload, 'expert', split_axis=0, concat_axis=0, tiled=True)  3.93 us
  transfers between devices with their start and end apart: 3, of which 1 were waited for; matrix products, arithmetic and copies ran while one was open for 0% of the time, Pallas kernels for 1%

profile of v5, /device:TPU:65, one launch (start us, length us, event | category | flops | bytes accessed | tf_op | source)
XLA Modules:
  0.0 123.0 jit_solution(2728700795494272852)
XLA Ops:
  0.0 43.4 %collective-permute-start = (bf16[640,1792]{1,0:T(8,128)(2,1)}, bf16[640,1792]{1,0:T(8,128)(2,1)S(1)}, u32[]{:S(2)}, u32[]{:S(2)}) collective-permute-start(bf16[640,1792]{1,0:T(8,128)(2,1)} %bitcast.11), channel_id=1, source_target_pairs={{0,1},{1,0},{2,3},{3,2},{4,5},{5,4},{6,7},{7,6},{8,9},{9,8},{10,11... | collective-permute-start | bytes 6881288 | tf_op jit(solution)/shard_map/ppermute | solution.py:171
  43.4 2.0 %collective-permute-start.1 = (bf16[160,3584]{1,0:T(8,128)(2,1)}, bf16[160,3584]{1,0:T(8,128)(2,1)S(1)}, u32[]{:S(2)}, u32[]{:S(2)}) collective-permute-start(bf16[160,3584]{1,0:T(8,128)(2,1)} %bitcast.13), channel_id=1, source_target_pairs={{0,1},{1,0},{2,3},{3,2},{4,5},{5,4},{6,7},{7,6},{8,9},{9,8},{10,11... | collective-permute-start | bytes 3440648 | tf_op jit(solution)/shard_map/ppermute | solution.py:172
  45.3 0.9 shard_map.64
  46.2 0.0 copy-start
  46.2 0.6 copy-done
  46.8 3.9 %all-to-all-start = ((bf16[16,8,256]{2,1,0:T(8,128)(2,1)}), bf16[16,8,256]{2,1,0:T(8,128)(2,1)S(1)}, u32[]{:S(2)}, u32[]{:S(2)}) async-start(bf16[16,8,256]{2,1,0:T(8,128)(2,1)} %copy-done), calls=%async_computation | async-start | bytes 131072 | tf_op jit(solution)/shard_map/all_to_all | solution.py:168
  50.8 11.2 %all-to-all-done = bf16[16,8,256]{2,1,0:T(8,128)(2,1)S(1)} async-done(((bf16[16,8,256]{2,1,0:T(8,128)(2,1)}), bf16[16,8,256]{2,1,0:T(8,128)(2,1)S(1)}, u32[]{:S(2)}, u32[]{:S(2)}) %all-to-all-start) | async-done | bytes 65568 | tf_op jit(solution)/shard_map/all_to_all | solution.py:168
  62.0 0.1 shard_map.65
  62.1 22.2 %all_gather.3.x_ref = bf16[3584,128]{1,0:T(8,128)(2,1)S(1)} all-gather(bf16[224,128]{1,0:T(8,128)(2,1)S(1)} %get-tuple-element.7), channel_id=1, replica_groups=mesh['groups'=2,'expert'=16,'split'=8,'pair'=2] {'split','pair'}, dimensions={0}, use_global_device_ids=true | all-gather | bytes 974848 | tf_op jit(solution)/shard_map/all_gather | solution.py:180
  84.3 0.0 collective-permute-done.1.down_other
  84.3 0.0 collective-permute-done.up_other
  84.4 3.3 %shard_map.66 = bf16[8,224,128]{2,1,0:T(8,128)(2,1)S(1)} custom-call(s32[1]{0:T(128)} %bitcast.pair_ref, bf16[3584,128]{1,0:T(8,128)(2,1)S(1)} %all_gather.3.x_ref, bf16[640,1792]{1,0:T(8,128)(2,1)} %bitcast.12, bf16[640,1792]{1,0:T(8,128)(2,1)S(1)} %collective-permute-done.up_other, f32[1,128]{1,0:T(1,128)S(1)} %get-tuple-element.8.weight_ref, ...), custom_call_target="tpu_custom_call" | custom-call | tf_op jit(solution)/shard_map/pallas_call | solution.py:134
  87.7 20.2 %all_to_all.15.parts_ref = bf16[8,224,128]{2,1,0:T(8,128)(2,1)S(1)} all-to-all(bf16[8,224,128]{2,1,0:T(8,128)(2,1)S(1)} %shard_map.66), channel_id=1, replica_groups=mesh['groups'=2,'expert'=16,'split'=8,'pair'=2] {'split'}, dimensions={0} | all-to-all | bytes 917504 | tf_op jit(solution)/shard_map/all_to_all | solution.py:194
  107.9 0.1 shard_map.67
  108.0 14.3 %all_to_all.16 = bf16[16,8,224]{2,1,0:T(8,128)(2,1)S(1)} all-to-all(bf16[16,8,224]{2,1,0:T(8,128)(2,1)S(1)} %bitcast.10), channel_id=1, replica_groups=mesh['groups'=2,'expert'=16,'split'=8,'pair'=2] {'expert'}, dimensions={0} | all-to-all | bytes 114688 | tf_op jit(solution)/shard_map/all_to_all | solution.py:196
  122.4 0.6 reduce_sum.12
Async XLA Ops:
  0.0 84.4 %collective-permute-start = (bf16[640,1792]{1,0:T(8,128)(2,1)}, bf16[640,1792]{1,0:T(8,128)(2,1)S(1)}, u32[]{:S(2)}, u32[]{:S(2)}) collective-permute-start(bf16[640,1792]{1,0:T(8,128)(2,1)} %bitcast.11), channel_id=1, source_target_pairs={{0,1},{1,0},{2,3},{3,2},{4,5},{5,4},{6,7},{7,6},{8,9},{9,8},{10,11... | collective-permute-start | bytes 6881288 | tf_op jit(solution)/shard_map/ppermute | solution.py:171
  43.4 41.0 %collective-permute-start.1 = (bf16[160,3584]{1,0:T(8,128)(2,1)}, bf16[160,3584]{1,0:T(8,128)(2,1)S(1)}, u32[]{:S(2)}, u32[]{:S(2)}) collective-permute-start(bf16[160,3584]{1,0:T(8,128)(2,1)} %bitcast.13), channel_id=1, source_target_pairs={{0,1},{1,0},{2,3},{3,2},{4,5},{5,4},{6,7},{7,6},{8,9},{9,8},{10,11... | collective-permute-start | bytes 3440648 | tf_op jit(solution)/shard_map/ppermute | solution.py:172
  46.2 0.6 copy-start
  46.8 15.2 %all-to-all-start = ((bf16[16,8,256]{2,1,0:T(8,128)(2,1)}), bf16[16,8,256]{2,1,0:T(8,128)(2,1)S(1)}, u32[]{:S(2)}, u32[]{:S(2)}) async-start(bf16[16,8,256]{2,1,0:T(8,128)(2,1)} %copy-done), calls=%async_computation | async-start | bytes 131072 | tf_op jit(solution)/shard_map/all_to_all | solution.py:168
